TPU v7x, 32 devices: a whole 2x2x4 slice. The times are simulated.
32 devices in a mesh: rep: 4 (over z), fsdp: 8 (over y, x, core).
Axes of the slice: x: 2, y: 2, z: 4, core: 2. Of those that a mesh axis runs over, the one named last changes fastest.
Arguments:
- hidden: bfloat16 [8192, 7168], P(('rep', 'fsdp')), may hold values from -6 to 6
- out_grad: bfloat16 [8192, 2048], P(('rep', 'fsdp')), may hold values from -0.125 to 0.125
- inner_params: float32 [4, 7168, 2048], P('rep', 'fsdp'), may hold values from -0.132 to 0.132
- first_moment: bfloat16 [4, 7168, 2048], P('rep', 'fsdp'), may hold values from -6 to 6
- second_moment: bfloat16 [4, 7168, 2048], P('rep', 'fsdp'), may hold values from 0.049804688 to 2
- outer_params: float32 [7168, 2048], P('fsdp', 'rep'), may hold values from -0.12 to 0.12
- outer_momentum: float32 [7168, 2048], P('fsdp', 'rep'), may hold values from -0.012 to 0.012
Outputs:
- new_params: float32 [7168, 2048], P('fsdp')
- new_momentum: float32 [7168, 2048], P('fsdp', 'rep')
- new_first: bfloat16 [4, 7168, 2048], P('rep', 'fsdp')
- new_second: bfloat16 [4, 7168, 2048], P('rep', 'fsdp')
All inputs are finite; a program needn't handle non-finite values.
Results may differ from a plain program's by a relative error of at most 0.009.
Values may be sent and summed in bfloat16 or wider, within the bound.
A program may use at most 192 MiB of HBM per device.

v0:
```python
import functools

import jax
import jax.numpy as jnp
from jax import lax
from jax.experimental import pallas as pl
from jax.experimental.pallas import tpu as pltpu
from jax.sharding import PartitionSpec as P

INNER_STEP = 500

beta_one = 0.9
beta_two = 0.95
epsilon = 1e-08
inner_rate = 0.0004
weight_decay = 0.1
outer_rate = 0.7
nesterov = 0.9

WIRE = jnp.bfloat16
WIRE_SCALE = 16.0


def encode(value):
    scaled = value * WIRE_SCALE
    square = scaled * scaled
    fourth = square * square
    eighth = fourth * fourth
    return jnp.where(scaled < 0.0, -eighth, eighth).astype(WIRE)


def decode(coded):
    wide = coded.astype(jnp.float32)
    root = jnp.sqrt(jnp.sqrt(jnp.sqrt(jnp.abs(wide)))) * (1.0 / WIRE_SCALE)
    return jnp.where(wide < 0.0, -root, root)


def outer_kernel(
    n, chunks, step_ref, outer_ref, mom_ref, out_ref, newmom_ref,
    from_left, from_right, acc, total,
    rs_send, rs_left, rs_right, ag_right, ag_left, ag_recv,
):
    z = lax.axis_index("rep")
    rows, block = outer_ref.shape
    rc = rows // chunks
    has_left, has_right = z > 0, z < n - 1

    barrier = pltpu.get_barrier_semaphore()

    @pl.when(has_left)
    def _():
        pl.semaphore_signal(barrier, inc=1, device_id={"rep": z - 1})

    @pl.when(has_right)
    def _():
        pl.semaphore_signal(barrier, inc=1, device_id={"rep": z + 1})

    pl.semaphore_wait(barrier, has_left.astype(jnp.int32) + has_right.astype(jnp.int32))

    def part(c, o):
        start = o * block
        if not isinstance(o, int):
            start = pl.multiple_of(start, 128)
        return pl.ds(pl.multiple_of(c * rc, rc), rc), pl.ds(start, block)

    def send_sum(src, c, o, to_right):
        at = part(c, o)
        return pltpu.make_async_remote_copy(
            src_ref=src.at[at],
            dst_ref=(from_left if to_right else from_right).at[at],
            send_sem=rs_send.at[c, o],
            recv_sem=(rs_left if to_right else rs_right).at[c, o],
            device_id={"rep": z + 1 if to_right else z - 1},
        )

    def send_new(c, o, to_right):
        at = part(c, o)
        return pltpu.make_async_remote_copy(
            src_ref=out_ref.at[at],
            dst_ref=out_ref.at[at],
            send_sem=(ag_right if to_right else ag_left).at[c, o],
            recv_sem=ag_recv.at[c, o],
            device_id={"rep": z + 1 if to_right else z - 1},
        )

    def wave(c, to_right):
        first = z == 0 if to_right else z == n - 1
        order = range(n - 1, 0, -1) if to_right else range(n - 1)
        for o in order:
            beyond = o > z if to_right else o < z
            at = part(c, o)

            @pl.when(jnp.logical_and(beyond, first))
            def _():
                acc[at] = encode(step_ref[at])
                send_sum(acc, c, o, to_right).start()

            @pl.when(jnp.logical_and(beyond, jnp.logical_not(first)))
            def _():
                send_sum(acc, c, o, to_right).wait_recv()
                came = (from_left if to_right else from_right)[at]
                acc[at] = encode(decode(came) + step_ref[at])
                send_sum(acc, c, o, to_right).start()

    def own(c):
        at = part(c, z)
        here = pl.ds(pl.multiple_of(c * rc, rc), rc)
        total[...] = step_ref[at]

        @pl.when(has_left)
        def _():
            send_sum(acc, c, z, True).wait_recv()
            total[...] += decode(from_left[at])

        @pl.when(has_right)
        def _():
            send_sum(acc, c, z, False).wait_recv()
            total[...] += decode(from_right[at])

        delta = outer_ref[here, :] - total[...] / n
        momentum = nesterov * mom_ref[here, :] + delta
        newmom_ref[here, :] = momentum
        updated = outer_ref[here, :] - outer_rate * (delta + nesterov * momentum)
        out_ref[at] = updated.astype(WIRE)

        @pl.when(has_right)
        def _():
            send_new(c, z, True).start()

        @pl.when(has_left)
        def _():
            send_new(c, z, False).start()

    def within(c, work):
        @pl.when(jnp.logical_and(c >= 0, c < chunks))
        def _():
            work(c)

    def own_lag(o):
        return jnp.maximum(o, n - 1 - o)

    def forward(t, distance, to_right):
        o = z - distance if to_right else z + distance
        there = o >= 0 if to_right else o < n
        c = t - own_lag(o) - distance
        ready = jnp.logical_and(there, jnp.logical_and(c >= 0, c < chunks))

        @pl.when(ready)
        def _():
            send_new(c, o, to_right).wait_recv()

        @pl.when(jnp.logical_and(ready, has_right if to_right else has_left))
        def _():
            send_new(c, o, to_right).start()

    def body(t, carry):
        within(t - z, lambda c: wave(c, True))
        within(t - (n - 1 - z), lambda c: wave(c, False))
        within(t - own_lag(z), own)
        for distance in range(1, n):
            forward(t, distance, True)
            forward(t, distance, False)
        return carry

    lax.fori_loop(0, chunks + 2 * (n - 1), body, 0)

    def drain(c, carry):
        for o in range(n):
            @pl.when(o > z)
            def _():
                send_sum(acc, c, o, True).wait_send()

            @pl.when(o < z)
            def _():
                send_sum(acc, c, o, False).wait_send()

            @pl.when(jnp.logical_and(o <= z, has_right))
            def _():
                send_new(c, o, True).wait_send()

            @pl.when(jnp.logical_and(o >= z, has_left))
            def _():
                send_new(c, o, False).wait_send()

        return carry

    lax.fori_loop(0, chunks, drain, 0)


def outer_step(stepped, outer_params, outer_momentum):
    n = lax.axis_size("rep")
    rows, block = outer_params.shape
    chunks = max(c for c in range(1, 15) if rows % (16 * c) == 0)
    vmem = pl.BlockSpec(memory_space=pltpu.VMEM)
    dma = pltpu.SemaphoreType.DMA((chunks, n))
    return pl.pallas_call(
        functools.partial(outer_kernel, n, chunks),
        out_shape=(
            jax.ShapeDtypeStruct(stepped.shape, WIRE),
            jax.ShapeDtypeStruct(outer_params.shape, jnp.float32),
        ),
        in_specs=[vmem] * 3,
        out_specs=(vmem, vmem),
        scratch_shapes=[
            pltpu.VMEM(stepped.shape, WIRE),
            pltpu.VMEM(stepped.shape, WIRE),
            pltpu.VMEM(stepped.shape, WIRE),
            pltpu.VMEM((rows // chunks, block), jnp.float32),
            dma, dma, dma, dma, dma, dma,
        ],
        compiler_params=pltpu.CompilerParams(
            collective_id=0, has_side_effects=True, vmem_limit_bytes=40 * 2**20
        ),
    )(stepped, outer_params, outer_momentum)


def per_device(
    hidden, out_grad, inner_params, first_moment, second_moment, outer_params, outer_momentum
):
    columns = lax.all_to_all(hidden, "fsdp", split_axis=1, concat_axis=0, tiled=True)
    segment = lax.all_gather(out_grad, "fsdp", axis=0, tiled=True)
    token_count = hidden.shape[0]
    blocks = segment.shape[0] // token_count
    gradient = jnp.einsum(
        "btf,btd->fd",
        columns.reshape(blocks, token_count, columns.shape[1]),
        segment.reshape(blocks, token_count, segment.shape[1]),
        preferred_element_type=jnp.float32,
    )
    stacked = gradient[None]
    moment_one = beta_one * first_moment.astype(jnp.float32) + (1.0 - beta_one) * stacked
    moment_two = beta_two * second_moment.astype(jnp.float32) + (1.0 - beta_two) * stacked * stacked
    corrected_one = moment_one / (1.0 - beta_one**INNER_STEP)
    corrected_two = moment_two / (1.0 - beta_two**INNER_STEP)
    stepped = inner_params - inner_rate * (
        corrected_one / (jnp.sqrt(corrected_two) + epsilon) + weight_decay * inner_params
    )
    gathered, new_momentum = outer_step(stepped[0], outer_params, outer_momentum)
    return (
        gathered.astype(jnp.float32),
        new_momentum,
        moment_one.astype(jnp.bfloat16),
        moment_two.astype(jnp.bfloat16),
    )


def solution(mesh):
    return jax.shard_map(
        per_device,
        mesh=mesh,
        in_specs=(
            P(("rep", "fsdp"), None),
            P(("rep", "fsdp"), None),
            P("rep", "fsdp", None),
            P("rep", "fsdp", None),
            P("rep", "fsdp", None),
            P("fsdp", "rep"),
            P("fsdp", "rep"),
        ),
        out_specs=(
            P("fsdp", None),
            P("fsdp", "rep"),
            P("rep", "fsdp", None),
            P("rep", "fsdp", None),
        ),
        check_vma=False,
    )
```

profile of v0, /device:TPU:0, one launch (start us, length us, event | category | flops | bytes accessed | tf_op | source)
XLA Modules:
  0.0 232.9 jit_solution(11387585317660952819)
XLA Ops:
  7.2 0.0 all-gather.2.cloned.1.call-start
  7.2 0.7 all-gather.2.cloned.1.call-update
  7.9 5.9 %copy.11 = bf16[256,7168]{0,1:T(8,128)(2,1)} copy(bf16[256,7168]{1,0:T(8,128)(2,1)} %param.7) | data formatting | bytes 7340032 | tf_op args[0]
  13.8 68.0 %all_to_all.16 = bf16[256,8,896]{0,2,1:T(8,128)(2,1)} all-to-all(bf16[256,8,896]{0,2,1:T(8,128)(2,1)} %bitcast.37), channel_id=1, replica_groups=mesh['rep'=4,'fsdp'=8] {'fsdp'}, dimensions={1} | all-to-all | bytes 7340032 | tf_op jit(solution)/shard_map/all_to_all | solution.py:220
  81.8 15.4 %all-gather.2.cloned.1.call-done = bf16[2048,2048]{1,0:T(8,128)(2,1)} async-done(((bf16[256,2048]{1,0:T(8,128)(2,1)}), bf16[2048,2048]{1,0:T(8,128)(2,1)}) %all-gather.2.cloned.1.call-update) | async-done | bytes 8388624 | tf_op jit(solution)/shard_map/all_gather | solution.py:221
  97.2 0.0 copy-start
  97.2 0.0 copy-start.1
  97.2 21.9 %fusion.5 = (bf16[1,896,2048]{2,1,0:T(8,128)(2,1)}, f32[896,2048]{1,0:T(8,128)}, bf16[1,896,2048]{2,1,0:T(8,128)(2,1)}) fusion(bf16[1,896,2048]{2,1,0:T(8,128)(2,1)} %param.11, f32[1,896,2048]{2,1,0:T(8,128)} %param.9, bf16[1,896,2048]{2,1,0:T(8,128)(2,1)} %param.10, bf16[8,256,2048]{2,1,0:T(8,128)(2,1)} %bitcast.38, bf16[256,8,896]{0,2,1:T(8,128)(2,1)} %all_to_all.16), kind=kOutput, calls=%fused_computation.9 | convolution fusion | flops 7547387904 | bytes 41418752 | tf_op jit(solution)/shard_map/btf,btd->fd/dot_general | solution.py:224
  119.1 0.0 copy-done
  119.1 0.0 copy-done.1
  119.1 101.7 %shard_map.102 = (bf16[896,2048]{1,0:T(8,128)(2,1)S(1)}, f32[896,512]{1,0:T(8,128)S(1)}) custom-call(f32[896,2048]{1,0:T(8,128)} %get-tuple-element.9.step_ref, f32[896,512]{1,0:T(8,128)S(1)} %copy-done, f32[896,512]{1,0:T(8,128)S(1)} %copy-done.1), custom_call_target="tpu_custom_call" | custom-call | tf_op jit(solution)/shard_map/pallas_call | solution.py:196
  220.9 4.0 %convert_element_type.17 = f32[896,2048]{1,0:T(8,128)} convert(bf16[896,2048]{1,0:T(8,128)(2,1)S(1)} %get-tuple-element.6) | non-fusion elementwise | flops 1835008 | bytes 11010048 | tf_op jit(solution)/shard_map/convert_element_type | solution.py:240
  224.9 1.2 copy.13
Async XLA Ops:
  7.2 90.0 %all-gather.2.cloned.1.call-start = ((), (), s32[]{:S(2)}) async-start(), calls=%async_computation.1 | async-start | bytes 9437184 | tf_op jit(solution)/shard_map/all_gather | solution.py:221
  97.2 21.9 %copy-start = (f32[896,512]{1,0:T(8,128)S(1)}, f32[896,512]{1,0:T(8,128)}, u32[]{:S(2)}) copy-start(f32[896,512]{1,0:T(8,128)} %outer_ref.1) | copy-start | bytes 5505028
  97.2 21.9 %copy-start.1 = (f32[896,512]{1,0:T(8,128)S(1)}, f32[896,512]{1,0:T(8,128)}, u32[]{:S(2)}) copy-start(f32[896,512]{1,0:T(8,128)} %mom_ref.1) | copy-start | bytes 5505028
Sparse Core Ops, SparseCore 0:
  9.9 87.3 all-gather.1
where the time goes:
time: 233 us
  Pallas kernels  102 us (44%)
  blocking collectives  68 us (29%)
  matrix products  21.9 us (9%)
  waiting for transfers between devices  16.1 us (7%)
  between operations  14 us (6%)
  local copies, waits for them, and re-layouts  7.15 us (3%)
  other arithmetic  3.99 us (2%)
    pallas_call x1, Pallas kernels, outer_step(): pl.pallas_call(functools.partial(outer_kernel, n, chunks), out_shape=(jax...  102 us
    all_to_all x1, blocking collectives, per_device(): lax.all_to_all(hidden, 'fsdp', split_axis=1, concat_axis=0, tiled=True)  68 us
    dot_general x1, matrix products, per_device(): jnp.einsum('btf,btd->fd', columns.reshape(blocks, token_count, columns.sh...  21.9 us
    all_gather x1, waiting for transfers between devices, per_device(): segment = lax.all_gather(out_grad, 'fsdp', axis=0, tiled=True)  15.4 us
    unnamed x6, local copies, waits for them, and re-layouts  7.15 us
  transfers between devices with their start and end apart: 1, of which 1 were waited for; matrix products, arithmetic and copies ran while one was open for 3% of the time, Pallas kernels for 0%

commit v1 on v0

--- a/solution.py
+++ b/solution.py
@@ -214,9 +214,423 @@
     )(stepped, outer_params, outer_momentum)
 
 
+ROW_TILE = 128
+COL_TILE = 256
+HOP_STEPS = 3
+AHEAD = 2
+SHELL_STEPS = 8
+CODE_RANGE = 560.0
+
+
+def fused_kernel(
+    cfg,
+    hid, og, par_hbm, first_hbm, second_hbm, outer_hbm, mom_hbm,
+    out_ref, newmom_ref, newfirst_ref, newsecond_ref,
+    hbuf, ht, obuf, step, first, second, outer, mom, acc, from_left, from_right,
+    h_send, h_recv, o_send, o_recv, sib_send, sib_recv, load_sem,
+    left_sem, right_sem, gather_sem, rs_send, ag_right, ag_left,
+):
+    n, peers, rows, width, tokens = cfg
+    ni, nj = rows // ROW_TILE, width // COL_TILE
+    stages = max(ni, nj)
+    halves = nj // n
+    chips = peers // 2
+    z = lax.axis_index("rep")
+    me = lax.axis_index("fsdp")
+    core, chip = me % 2, me // 2
+    has_left, has_right = z > 0, z < n - 1
+
+    def flag(condition):
+        return condition.astype(jnp.int32)
+
+    def peer_chip(d):
+        return ((chip // 2 + d // 2) % (chips // 2)) * 2 + (chip + d) % 2
+
+    sibling = chip * 2 + 1 - core
+
+    barrier = pltpu.get_barrier_semaphore()
+    for d in range(1, peers):
+        target = peer_chip(d // 2) * 2 + (core + d) % 2
+        pl.semaphore_signal(barrier, inc=1, device_id={"fsdp": target})
+
+    @pl.when(has_left)
+    def _():
+        pl.semaphore_signal(barrier, inc=1, device_id={"rep": z - 1})
+
+    @pl.when(has_right)
+    def _():
+        pl.semaphore_signal(barrier, inc=1, device_id={"rep": z + 1})
+
+    pl.semaphore_wait(barrier, peers - 1 + flag(has_left) + flag(has_right))
+
+    counts = [
+        (ni if s >= ni else nj if s >= nj else 2 * s + 1) for s in range(stages)
+    ]
+    widths = [max(c, SHELL_STEPS) if s < stages - 1 else c for s, c in enumerate(counts)]
+    starts = [sum(widths[:s]) for s in range(stages + 1)]
+    total_steps = starts[-1]
+
+    def chunk_of(j):
+        return (j + (n - 1) * halves) % nj
+
+    def own_lag(o):
+        return max(o, n - 1 - o) if isinstance(o, int) else jnp.maximum(o, n - 1 - o)
+
+    def place(u):
+        s = jnp.int32(0)
+        base = jnp.int32(0)
+        for a, b in zip(starts[:-2], starts[1:-1]):
+            past = flag(u >= b)
+            s = s + past
+            base = base + past * (b - a)
+        return s, u - base
+
+    def tile(u):
+        s, q = place(u)
+        low = q < s
+        i = jnp.where(low, q, s)
+        j = jnp.where(low, s, q - s)
+        count = jnp.where(s >= ni, ni, 2 * s + 1)
+        valid = (u >= 0) & (u < total_steps) & (q < count)
+        return valid, i, j, chunk_of(j)
+
+    def rows_of(i):
+        return pl.ds(pl.multiple_of(i * ROW_TILE, ROW_TILE), ROW_TILE)
+
+    def cols_of(c):
+        return pl.ds(pl.multiple_of(c * COL_TILE, COL_TILE), COL_TILE)
+
+    def hid_cols(owner, s):
+        return pl.ds(pl.multiple_of(owner * rows + s * ROW_TILE, ROW_TILE), ROW_TILE)
+
+    def send_o(s, d):
+        return pltpu.make_async_remote_copy(
+            src_ref=og.at[:, cols_of(chunk_of(s))],
+            dst_ref=obuf.at[s, me],
+            send_sem=o_send.at[s],
+            recv_sem=o_recv.at[s, chip],
+            device_id={"fsdp": peer_chip(d) * 2 + core},
+        )
+
+    def issue_o(s):
+        for d in range(1, chips):
+            send_o(s, d).start()
+        pltpu.make_async_remote_copy(
+            src_ref=og.at[:, cols_of(chunk_of(s))],
+            dst_ref=obuf.at[s, me],
+            send_sem=sib_send.at[s],
+            recv_sem=sib_recv.at[s],
+            device_id={"fsdp": sibling},
+        ).start()
+        pltpu.make_async_copy(
+            og.at[:, cols_of(chunk_of(s))], obuf.at[s, me], o_recv.at[s, chip]
+        ).start()
+
+    def forward_o(s):
+        for d in range(chips):
+            source = peer_chip(d)
+            block = source * 2 + core
+            pltpu.make_async_copy(
+                obuf.at[s, block], obuf.at[s, block], o_recv.at[s, source]
+            ).wait()
+            if d > 0:
+                pltpu.make_async_remote_copy(
+                    src_ref=obuf.at[s, block],
+                    dst_ref=obuf.at[s, block],
+                    send_sem=sib_send.at[s],
+                    recv_sem=sib_recv.at[s],
+                    device_id={"fsdp": sibling},
+                ).start()
+
+    def issue_h(s):
+        for d in list(range(2, peers)) + [1]:
+            target = peer_chip(d // 2) * 2 + (core + d) % 2
+            pltpu.make_async_remote_copy(
+                src_ref=hid.at[:, hid_cols(target, s)],
+                dst_ref=hbuf.at[s, me],
+                send_sem=h_send.at[s],
+                recv_sem=h_recv.at[s],
+                device_id={"fsdp": target},
+            ).start()
+        pltpu.make_async_copy(
+            hid.at[:, hid_cols(me, s)], hbuf.at[s, me], h_recv.at[s]
+        ).start()
+
+    def issue(s):
+        if isinstance(s, int):
+            if s < nj:
+                issue_o(s)
+            if s < ni:
+                issue_h(s)
+        else:
+            @pl.when(s < nj)
+            def _():
+                issue_o(s)
+
+            @pl.when(s < ni)
+            def _():
+                issue_h(s)
+
+    for s in range(AHEAD):
+        issue(s)
+    loads = [
+        pltpu.make_async_copy(a, b, load_sem.at[k])
+        for k, (a, b) in enumerate(
+            ((par_hbm, step), (first_hbm, first), (second_hbm, second), (outer_hbm, outer), (mom_hbm, mom))
+        )
+    ]
+    for load in loads:
+        load.start()
+
+    def code_scale(terms):
+        return CODE_RANGE / terms.astype(jnp.float32)
+
+    def encode(value, terms):
+        return jnp.exp(value * code_scale(terms)).astype(WIRE)
+
+    def decode(coded, terms):
+        return jnp.log(coded.astype(jnp.float32)) * (1.0 / code_scale(terms))
+
+    def send_sum(i, j, o, to_right):
+        return pltpu.make_async_remote_copy(
+            src_ref=acc.at[i, j],
+            dst_ref=(from_left if to_right else from_right).at[i, j],
+            send_sem=rs_send.at[o],
+            recv_sem=(left_sem if to_right else right_sem).at[i, j],
+            device_id={"rep": z + 1 if to_right else z - 1},
+        )
+
+    def send_new(i, j, c, to_right):
+        at = rows_of(i), cols_of(c)
+        return pltpu.make_async_remote_copy(
+            src_ref=out_ref.at[at],
+            dst_ref=out_ref.at[at],
+            send_sem=(ag_right if to_right else ag_left).at[c // halves],
+            recv_sem=gather_sem.at[i, j],
+            device_id={"rep": z + 1 if to_right else z - 1},
+        )
+
+    def wave(t, to_right):
+        hop = z if to_right else n - 1 - z
+        valid, i, j, c = tile(t - hop * HOP_STEPS)
+        o = c // halves
+        beyond = (o > z) if to_right else (o < z)
+        at = rows_of(i), cols_of(c)
+        active = valid & beyond
+
+        @pl.when(active & (hop == 0))
+        def _():
+            acc[i, j] = encode(step[at], hop + 1)
+            send_sum(i, j, o, to_right).start()
+
+        @pl.when(active & (hop > 0))
+        def _():
+            send_sum(i, j, o, to_right).wait_recv()
+            came = (from_left if to_right else from_right)[i, j]
+            acc[i, j] = encode(decode(came, hop) + step[at], hop + 1)
+            send_sum(i, j, o, to_right).start()
+
+    def own(t):
+        valid, i, j, c = tile(t - own_lag(z) * HOP_STEPS)
+
+        @pl.when(valid & (c // halves == z))
+        def _():
+            at = rows_of(i), cols_of(c)
+            local = rows_of(i), cols_of(c % halves)
+
+            @pl.when(has_left)
+            def _():
+                send_sum(i, j, z, True).wait_recv()
+                step[at] += decode(from_left[i, j], z)
+
+            @pl.when(has_right)
+            def _():
+                send_sum(i, j, z, False).wait_recv()
+                step[at] += decode(from_right[i, j], n - 1 - z)
+
+            delta = outer[local] - step[at] * (1.0 / n)
+            momentum = nesterov * mom[local] + delta
+            newmom_ref[local] = momentum
+            updated = outer[local] - outer_rate * (delta + nesterov * momentum)
+            out_ref[at] = updated.astype(WIRE)
+
+            @pl.when(has_right)
+            def _():
+                send_new(i, j, c, True).start()
+
+            @pl.when(has_left)
+            def _():
+                send_new(i, j, c, False).start()
+
+    def pass_on(t, e):
+        o = (z + e) % n
+        to_right = o < z
+        distance = jnp.where(to_right, z - o, o - z)
+        valid, i, j, c = tile(t - (own_lag(o) + distance) * HOP_STEPS)
+        ready = valid & (c // halves == o)
+
+        @pl.when(ready)
+        def _():
+            send_new(i, j, c, True).wait_recv()
+
+            @pl.when(to_right & has_right)
+            def _():
+                send_new(i, j, c, True).start()
+
+            @pl.when((o > z) & has_left)
+            def _():
+                send_new(i, j, c, False).start()
+
+    def compute(t):
+        s, q = place(t)
+        valid, i, j, c = tile(t)
+
+        @pl.when((q == 0) & (t < total_steps))
+        def _():
+            issue(s + AHEAD)
+
+            @pl.when(s < ni)
+            def _():
+                pltpu.make_async_copy(hbuf.at[s], hbuf.at[s], h_recv.at[s]).wait()
+                ht[s] = hbuf[s].reshape(peers * tokens, ROW_TILE).T
+
+            @pl.when(s < nj)
+            def _():
+                four = obuf.at[s, pl.ds(0, chips)]
+                pltpu.make_async_copy(four, four, sib_recv.at[s]).wait()
+
+        @pl.when((q == SHELL_STEPS // 2) & (s + 1 < nj) & (t < total_steps))
+        def _():
+            forward_o(s + 1)
+
+        @pl.when(valid)
+        def _():
+            at = rows_of(i), cols_of(c)
+            gradient = jnp.dot(
+                ht[i],
+                obuf[j].reshape(peers * tokens, COL_TILE),
+                preferred_element_type=jnp.float32,
+            )
+            one = beta_one * first[at].astype(jnp.float32) + (1.0 - beta_one) * gradient
+            two = beta_two * second[at].astype(jnp.float32) + (1.0 - beta_two) * gradient * gradient
+            newfirst_ref[at] = one.astype(jnp.bfloat16)
+            newsecond_ref[at] = two.astype(jnp.bfloat16)
+            corrected_one = one * (1.0 / (1.0 - beta_one**INNER_STEP))
+            corrected_two = two * (1.0 / (1.0 - beta_two**INNER_STEP))
+            held = step[at]
+            step[at] = held - inner_rate * (
+                corrected_one / (jnp.sqrt(corrected_two) + epsilon) + weight_decay * held
+            )
+
+    forward_o(0)
+    for load in loads:
+        load.wait()
+
+    last = 0
+    for s, c in enumerate(counts):
+        for q in range(c):
+            j = q if s >= nj else (s if q < s else q - s)
+            o = ((j + (n - 1) * halves) % nj) // halves
+            lag = own_lag(o) + max(o, n - 1 - o)
+            last = max(last, starts[s] + q + lag * HOP_STEPS)
+
+    def body(t, carry):
+        for e in range(1, n):
+            pass_on(t, e)
+        own(t)
+        compute(t)
+        wave(t, True)
+        wave(t, False)
+        return carry
+
+    lax.fori_loop(0, last + 1, body, 0)
+
+    for o in range(n):
+        part = acc.at[:, pl.ds(0, halves)]
+
+        @pl.when(z != o)
+        def _():
+            pltpu.make_async_copy(part, part, rs_send.at[o]).wait()
+
+        @pl.when((o <= z) & has_right)
+        def _():
+            pltpu.make_async_copy(part, part, ag_right.at[o]).wait()
+
+        @pl.when((o >= z) & has_left)
+        def _():
+            pltpu.make_async_copy(part, part, ag_left.at[o]).wait()
+
+    for s in range(ni):
+        sent = hbuf.at[s, pl.ds(0, peers - 1)]
+        pltpu.make_async_copy(sent, sent, h_send.at[s]).wait()
+    for s in range(nj):
+        sent = obuf.at[s, pl.ds(0, chips - 1)]
+        pltpu.make_async_copy(sent, sent, o_send.at[s]).wait()
+        sent = obuf.at[s, pl.ds(0, chips)]
+        pltpu.make_async_copy(sent, sent, sib_send.at[s]).wait()
+
+
+def fused(hidden, out_grad, inner_params, first_moment, second_moment, outer_params, outer_momentum):
+    n, peers = lax.axis_size("rep"), lax.axis_size("fsdp")
+    tokens = hidden.shape[0]
+    rows, width = inner_params.shape
+    block = outer_params.shape[1]
+    ni, nj = rows // ROW_TILE, width // COL_TILE
+    cfg = (n, peers, rows, width, tokens)
+    anywhere = pl.BlockSpec(memory_space=pl.ANY)
+    vmem = pl.BlockSpec(memory_space=pltpu.VMEM)
+    dma = pltpu.SemaphoreType.DMA
+    bf16, f32 = jnp.bfloat16, jnp.float32
+    return pl.pallas_call(
+        functools.partial(fused_kernel, cfg),
+        out_shape=(
+            jax.ShapeDtypeStruct((rows, width), WIRE),
+            jax.ShapeDtypeStruct((rows, block), f32),
+            jax.ShapeDtypeStruct((rows, width), bf16),
+            jax.ShapeDtypeStruct((rows, width), bf16),
+        ),
+        in_specs=[anywhere] * 7,
+        out_specs=(vmem,) * 4,
+        scratch_shapes=[
+            pltpu.VMEM((ni, peers, tokens, ROW_TILE), bf16),
+            pltpu.VMEM((ni, ROW_TILE, peers * tokens), bf16),
+            pltpu.VMEM((nj, peers, tokens, COL_TILE), bf16),
+            pltpu.VMEM((rows, width), f32),
+            pltpu.VMEM((rows, width), bf16),
+            pltpu.VMEM((rows, width), bf16),
+            pltpu.VMEM((rows, block), f32),
+            pltpu.VMEM((rows, block), f32),
+            pltpu.VMEM((ni, nj, ROW_TILE, COL_TILE), WIRE),
+            pltpu.VMEM((ni, nj, ROW_TILE, COL_TILE), WIRE),
+            pltpu.VMEM((ni, nj, ROW_TILE, COL_TILE), WIRE),
+            dma((ni,)), dma((ni,)),
+            dma((nj,)), dma((nj, peers // 2)), dma((nj,)), dma((nj,)), dma((5,)),
+            dma((ni, nj)), dma((ni, nj)), dma((ni, nj)),
+            dma((n,)), dma((n,)), dma((n,)),
+        ],
+        compiler_params=pltpu.CompilerParams(
+            collective_id=1, has_side_effects=True, vmem_limit_bytes=67043328
+        ),
+    )(hidden, out_grad, inner_params, first_moment, second_moment, outer_params, outer_momentum)
+
+
+def fits(peers, n, rows, width, block, tokens):
+    if peers % 4 or rows % ROW_TILE or block % COL_TILE or tokens % 16:
+        return False
+    return rows // ROW_TILE <= width // COL_TILE
+
+
 def per_device(
     hidden, out_grad, inner_params, first_moment, second_moment, outer_params, outer_momentum
 ):
+    rows, width = inner_params.shape[1:]
+    block, tokens = outer_params.shape[1], hidden.shape[0]
+    if fits(lax.axis_size("fsdp"), lax.axis_size("rep"), rows, width, block, tokens):
+        gathered, new_momentum, new_first, new_second = fused(
+            hidden, out_grad, inner_params[0], first_moment[0], second_moment[0],
+            outer_params, outer_momentum,
+        )
+        return gathered.astype(jnp.float32), new_momentum, new_first[None], new_second[None]
     columns = lax.all_to_all(hidden, "fsdp", split_axis=1, concat_axis=0, tiled=True)
     segment = lax.all_gather(out_grad, "fsdp", axis=0, tiled=True)
     token_count = hidden.shape[0]

time: 233 us -> 169 us (0.73)
  blocking collectives: 68 us -> 0 us
  Pallas kernels: 102 us -> 154 us
  matrix products: 21.9 us -> 0 us
  waiting for transfers between devices: 16.1 us -> 0 us
  between operations: 14 us -> 0.65 us
    all_to_all x1 -> x0, blocking collectives: 68 us -> none  [per_device(): lax.all_to_all(hidden, 'fsdp', split_axis=1, concat_axis=0, tiled=True)]
    pallas_call x1, Pallas kernels: 102 us -> 154 us  [fused(): pl.pallas_call(functools.partial(fused_kernel, cfg), out_shape=(jax.Shape...]
    dot_general x1 -> x0, matrix products: 21.9 us -> none  [per_device(): jnp.einsum('btf,btd->fd', columns.reshape(blocks, token_count, columns.sh...]
    all_gather x1 -> x0, waiting for transfers between devices: 15.4 us -> none  [per_device(): segment = lax.all_gather(out_grad, 'fsdp', axis=0, tiled=True)]
    unnamed x6 -> x9, local copies, waits for them, and re-layouts: 7.15 us -> 7.9 us
  transfers between devices with their start and end apart: 1 -> 0, of which waited for: 1 -> 0; matrix products, arithmetic and copies ran while one was open for 3% -> 0% of each run, Pallas kernels for 0% -> 0%
where the time goes in v1:
time: 169 us
  Pallas kernels  154 us (91%)
  local copies, waits for them, and re-layouts  7.9 us (5%)
  other arithmetic  6.15 us (4%)
    pallas_call x1, Pallas kernels, fused(): pl.pallas_call(functools.partial(fused_kernel, cfg), out_shape=(jax.Shape...  154 us
    unnamed x9, local copies, waits for them, and re-layouts  7.9 us
    convert_element_type x1, other arithmetic, per_device(): gathered.astype(jnp.float32)  6.15 us

profile of v1, /device:TPU:0, one launch (start us, length us, event | category | flops | bytes accessed | tf_op | source)
XLA Modules:
  0.0 168.8 jit_solution(6109896107638147057)
XLA Ops:
  0.6 154.1 %shard_map.102 = (bf16[896,2048]{1,0:T(8,128)(2,1)}, f32[896,512]{1,0:T(8,128)}, bf16[896,2048]{1,0:T(8,128)(2,1)}, bf16[896,2048]{1,0:T(8,128)(2,1)}) custom-call(bf16[256,7168]{1,0:T(8,128)(2,1)} %hid.1, bf16[256,2048]{1,0:T(8,128)(2,1)} %og.1, f32[896,2048]{1,0:T(8,128)} %bitcast.5, bf16[896,2048]{1,0:T(8,128)(2,1)} %bitcast.8, ...), custom_call_target="tpu_custom_call" | custom-call | tf_op jit(solution)/shard_map/pallas_call | solution.py:584
  154.8 0.0 copy-start.2
  154.8 6.2 %convert_element_type.3 = f32[896,2048]{1,0:T(8,128)} convert(bf16[896,2048]{1,0:T(8,128)(2,1)} %get-tuple-element.8) | non-fusion elementwise | flops 1835008 | bytes 11010048 | tf_op jit(solution)/shard_map/convert_element_type | solution.py:633
  160.9 0.0 copy-done.2
  160.9 0.0 copy-start.1
  160.9 1.2 copy.14
  162.1 1.5 copy-done.1
  163.6 0.0 copy-start
  163.6 1.9 %copy.15 = bf16[1,896,2048]{2,1,0:T(8,128)(2,1)} copy(bf16[1,896,2048]{2,1,0:T(8,128)(2,1)S(1)} %bitcast.7) | data formatting | bytes 7340032
  165.5 1.5 copy-done
  167.0 1.8 %copy.16 = bf16[1,896,2048]{2,1,0:T(8,128)(2,1)} copy(bf16[1,896,2048]{2,1,0:T(8,128)(2,1)S(1)} %bitcast.6) | data formatting | bytes 7340032
Async XLA Ops:
  154.8 6.2 %copy-start.2 = (f32[896,512]{1,0:T(8,128)S(1)}, f32[896,512]{1,0:T(8,128)}, u32[]{:S(2)}) copy-start(f32[896,512]{1,0:T(8,128)} %get-tuple-element.17) | copy-start | bytes 5505028
  160.9 2.7 %copy-start.1 = (bf16[896,2048]{1,0:T(8,128)(2,1)S(1)}, bf16[896,2048]{1,0:T(8,128)(2,1)}, u32[]{:S(2)}) copy-start(bf16[896,2048]{1,0:T(8,128)(2,1)} %get-tuple-element.10) | copy-start | bytes 11010052
  163.6 3.4 %copy-start = (bf16[896,2048]{1,0:T(8,128)(2,1)S(1)}, bf16[896,2048]{1,0:T(8,128)(2,1)}, u32[]{:S(2)}) copy-start(bf16[896,2048]{1,0:T(8,128)(2,1)} %get-tuple-element.11) | copy-start | bytes 11010052

commit v2 on v1

--- a/solution.py
+++ b/solution.py
@@ -215,18 +215,21 @@
 
 
 ROW_TILE = 128
+VMEM_BYTES = 40000000
 COL_TILE = 256
-HOP_STEPS = 3
+HOP_STEPS = 5
 AHEAD = 2
-SHELL_STEPS = 8
+SEGMENT_STEPS = 6
+LEAD = 1
+EDGE_LAG = 3
 CODE_RANGE = 560.0
 
 
 def fused_kernel(
     cfg,
     hid, og, par_hbm, first_hbm, second_hbm, outer_hbm, mom_hbm,
-    out_ref, newmom_ref, newfirst_ref, newsecond_ref,
-    hbuf, ht, obuf, step, first, second, outer, mom, acc, from_left, from_right,
+    wide_ref, mom, first, second,
+    hbuf, ht, obuf, step, outer, out_ref, from_left, from_right,
     h_send, h_recv, o_send, o_recv, sib_send, sib_recv, load_sem,
     left_sem, right_sem, gather_sem, rs_send, ag_right, ag_left,
 ):
@@ -263,11 +266,14 @@
 
     pl.semaphore_wait(barrier, peers - 1 + flag(has_left) + flag(has_right))
 
-    counts = [
-        (ni if s >= ni else nj if s >= nj else 2 * s + 1) for s in range(stages)
+    segments = ni + nj - 1
+    counts = [(g + 2) // 2 for g in range(segments)]
+    leads = [LEAD * (g % 2) for g in range(segments)]
+    widths = [
+        max(c + a, SEGMENT_STEPS) if g < segments - 1 else c + a
+        for g, (c, a) in enumerate(zip(counts, leads))
     ]
-    widths = [max(c, SHELL_STEPS) if s < stages - 1 else c for s, c in enumerate(counts)]
-    starts = [sum(widths[:s]) for s in range(stages + 1)]
+    starts = [sum(widths[:g]) for g in range(segments + 1)]
     total_steps = starts[-1]
 
     def chunk_of(j):
@@ -277,21 +283,22 @@
         return max(o, n - 1 - o) if isinstance(o, int) else jnp.maximum(o, n - 1 - o)
 
     def place(u):
-        s = jnp.int32(0)
+        g = jnp.int32(0)
         base = jnp.int32(0)
         for a, b in zip(starts[:-2], starts[1:-1]):
             past = flag(u >= b)
-            s = s + past
+            g = g + past
             base = base + past * (b - a)
-        return s, u - base
+        return g, u - base
 
     def tile(u):
-        s, q = place(u)
-        low = q < s
-        i = jnp.where(low, q, s)
-        j = jnp.where(low, s, q - s)
-        count = jnp.where(s >= ni, ni, 2 * s + 1)
-        valid = (u >= 0) & (u < total_steps) & (q < count)
+        g, q = place(u)
+        odd = g % 2
+        half = (g + 1) // 2
+        q = q - LEAD * odd
+        i = jnp.where(odd == 1, q, half)
+        j = jnp.where(odd == 1, half, q)
+        valid = (u >= 0) & (u < total_steps) & (q >= 0) & (q < half + 1 - odd)
         return valid, i, j, chunk_of(j)
 
     def rows_of(i):
@@ -342,6 +349,10 @@
                     device_id={"fsdp": sibling},
                 ).start()
 
+    def gathered_o(s):
+        four = obuf.at[s, pl.ds(0, chips)]
+        pltpu.make_async_copy(four, four, sib_recv.at[s]).wait()
+
     def issue_h(s):
         for d in list(range(2, peers)) + [1]:
             target = peer_chip(d // 2) * 2 + (core + d) % 2
@@ -393,7 +404,7 @@
 
     def send_sum(i, j, o, to_right):
         return pltpu.make_async_remote_copy(
-            src_ref=acc.at[i, j],
+            src_ref=(from_left if to_right else from_right).at[i, j],
             dst_ref=(from_left if to_right else from_right).at[i, j],
             send_sem=rs_send.at[o],
             recv_sem=(left_sem if to_right else right_sem).at[i, j],
@@ -417,17 +428,17 @@
         beyond = (o > z) if to_right else (o < z)
         at = rows_of(i), cols_of(c)
         active = valid & beyond
+        partial = from_left if to_right else from_right
 
         @pl.when(active & (hop == 0))
         def _():
-            acc[i, j] = encode(step[at], hop + 1)
+            partial[i, j] = encode(step[at], hop + 1)
             send_sum(i, j, o, to_right).start()
 
         @pl.when(active & (hop > 0))
         def _():
             send_sum(i, j, o, to_right).wait_recv()
-            came = (from_left if to_right else from_right)[i, j]
-            acc[i, j] = encode(decode(came, hop) + step[at], hop + 1)
+            partial[i, j] = encode(decode(partial[i, j], hop) + step[at], hop + 1)
             send_sum(i, j, o, to_right).start()
 
     def own(t):
@@ -450,9 +461,10 @@
 
             delta = outer[local] - step[at] * (1.0 / n)
             momentum = nesterov * mom[local] + delta
-            newmom_ref[local] = momentum
+            mom[local] = momentum
             updated = outer[local] - outer_rate * (delta + nesterov * momentum)
             out_ref[at] = updated.astype(WIRE)
+            wide_ref[at] = updated
 
             @pl.when(has_right)
             def _():
@@ -466,8 +478,11 @@
         o = (z + e) % n
         to_right = o < z
         distance = jnp.where(to_right, z - o, o - z)
-        valid, i, j, c = tile(t - (own_lag(o) + distance) * HOP_STEPS)
+        edge = jnp.where(to_right, flag(has_right), flag(has_left)) == 0
+        lag = (own_lag(o) + distance) * HOP_STEPS + EDGE_LAG * flag(edge)
+        valid, i, j, c = tile(t - lag)
         ready = valid & (c // halves == o)
+        at = rows_of(i), cols_of(c)
 
         @pl.when(ready)
         def _():
@@ -481,27 +496,27 @@
             def _():
                 send_new(i, j, c, False).start()
 
+            wide_ref[at] = out_ref[at].astype(jnp.float32)
+
     def compute(t):
-        s, q = place(t)
+        g, q = place(t)
+        s = (g + 1) // 2
+        inside = t < total_steps
         valid, i, j, c = tile(t)
 
-        @pl.when((q == 0) & (t < total_steps))
+        @pl.when(inside & (g % 2 == 0) & (q == 0))
         def _():
             issue(s + AHEAD)
-
-            @pl.when(s < ni)
-            def _():
-                pltpu.make_async_copy(hbuf.at[s], hbuf.at[s], h_recv.at[s]).wait()
-                ht[s] = hbuf[s].reshape(peers * tokens, ROW_TILE).T
-
-            @pl.when(s < nj)
-            def _():
-                four = obuf.at[s, pl.ds(0, chips)]
-                pltpu.make_async_copy(four, four, sib_recv.at[s]).wait()
-
-        @pl.when((q == SHELL_STEPS // 2) & (s + 1 < nj) & (t < total_steps))
-        def _():
-            forward_o(s + 1)
+            pltpu.make_async_copy(hbuf.at[s], hbuf.at[s], h_recv.at[s]).wait()
+            ht[s] = hbuf[s].reshape(peers * tokens, ROW_TILE).T
+
+        @pl.when(inside & (g % 2 == 1) & (q == 0))
+        def _():
+            forward_o(s)
+
+        @pl.when(inside & (g % 2 == 1) & (q == LEAD))
+        def _():
+            gathered_o(s)
 
         @pl.when(valid)
         def _():
@@ -513,8 +528,8 @@
             )
             one = beta_one * first[at].astype(jnp.float32) + (1.0 - beta_one) * gradient
             two = beta_two * second[at].astype(jnp.float32) + (1.0 - beta_two) * gradient * gradient
-            newfirst_ref[at] = one.astype(jnp.bfloat16)
-            newsecond_ref[at] = two.astype(jnp.bfloat16)
+            first[at] = one.astype(jnp.bfloat16)
+            second[at] = two.astype(jnp.bfloat16)
             corrected_one = one * (1.0 / (1.0 - beta_one**INNER_STEP))
             corrected_two = two * (1.0 / (1.0 - beta_two**INNER_STEP))
             held = step[at]
@@ -525,14 +540,15 @@
     forward_o(0)
     for load in loads:
         load.wait()
+    gathered_o(0)
 
     last = 0
-    for s, c in enumerate(counts):
+    for g, c in enumerate(counts):
         for q in range(c):
-            j = q if s >= nj else (s if q < s else q - s)
-            o = ((j + (n - 1) * halves) % nj) // halves
-            lag = own_lag(o) + max(o, n - 1 - o)
-            last = max(last, starts[s] + q + lag * HOP_STEPS)
+            j = (g + 1) // 2 if g % 2 else q
+            o = chunk_of(j) // halves
+            hops = own_lag(o) + max(o, n - 1 - o)
+            last = max(last, starts[g] + leads[g] + q + hops * HOP_STEPS + EDGE_LAG)
 
     def body(t, carry):
         for e in range(1, n):
@@ -546,7 +562,7 @@
     lax.fori_loop(0, last + 1, body, 0)
 
     for o in range(n):
-        part = acc.at[:, pl.ds(0, halves)]
+        part = from_left.at[:, pl.ds(0, halves)]
 
         @pl.when(z != o)
         def _():
@@ -584,10 +600,10 @@
     return pl.pallas_call(
         functools.partial(fused_kernel, cfg),
         out_shape=(
-            jax.ShapeDtypeStruct((rows, width), WIRE),
-            jax.ShapeDtypeStruct((rows, block), f32),
-            jax.ShapeDtypeStruct((rows, width), bf16),
-            jax.ShapeDtypeStruct((rows, width), bf16),
+            pltpu.VMEM((rows, width), f32),
+            pltpu.VMEM((rows, block), f32),
+            pltpu.VMEM((rows, width), bf16),
+            pltpu.VMEM((rows, width), bf16),
         ),
         in_specs=[anywhere] * 7,
         out_specs=(vmem,) * 4,
@@ -596,11 +612,8 @@
             pltpu.VMEM((ni, ROW_TILE, peers * tokens), bf16),
             pltpu.VMEM((nj, peers, tokens, COL_TILE), bf16),
             pltpu.VMEM((rows, width), f32),
-            pltpu.VMEM((rows, width), bf16),
-            pltpu.VMEM((rows, width), bf16),
             pltpu.VMEM((rows, block), f32),
-            pltpu.VMEM((rows, block), f32),
-            pltpu.VMEM((ni, nj, ROW_TILE, COL_TILE), WIRE),
+            pltpu.VMEM((rows, width), WIRE),
             pltpu.VMEM((ni, nj, ROW_TILE, COL_TILE), WIRE),
             pltpu.VMEM((ni, nj, ROW_TILE, COL_TILE), WIRE),
             dma((ni,)), dma((ni,)),
@@ -609,7 +622,7 @@
             dma((n,)), dma((n,)), dma((n,)),
         ],
         compiler_params=pltpu.CompilerParams(
-            collective_id=1, has_side_effects=True, vmem_limit_bytes=67043328
+            collective_id=1, has_side_effects=True, vmem_limit_bytes=VMEM_BYTES
         ),
     )(hidden, out_grad, inner_params, first_moment, second_moment, outer_params, outer_momentum)
 
@@ -617,7 +630,7 @@
 def fits(peers, n, rows, width, block, tokens):
     if peers % 4 or rows % ROW_TILE or block % COL_TILE or tokens % 16:
         return False
-    return rows // ROW_TILE <= width // COL_TILE
+    return 0 <= width // COL_TILE - rows // ROW_TILE <= 1
 
 
 def per_device(
@@ -630,7 +643,7 @@
             hidden, out_grad, inner_params[0], first_moment[0], second_moment[0],
             outer_params, outer_momentum,
         )
-        return gathered.astype(jnp.float32), new_momentum, new_first[None], new_second[None]
+        return gathered, new_momentum, new_first[None], new_second[None]
     columns = lax.all_to_all(hidden, "fsdp", split_axis=1, concat_axis=0, tiled=True)
     segment = lax.all_gather(out_grad, "fsdp", axis=0, tiled=True)
     token_count = hidden.shape[0]

time: 169 us -> 153 us (0.905)
  Pallas kernels: 154 us -> 145 us
  other arithmetic: 6.15 us -> 0 us
    pallas_call x1, Pallas kernels: 154 us -> 145 us  [fused(): pl.pallas_call(functools.partial(fused_kernel, cfg), out_shape=(pltpu.VME...]
    convert_element_type x1 -> x0, other arithmetic: 6.15 us -> none  [per_device(): gathered.astype(jnp.float32)]
    unnamed x9 -> x4, local copies, waits for them, and re-layouts: 7.9 us -> 7.95 us
where the time goes in v2:
time: 153 us
  Pallas kernels  145 us (95%)
  local copies, waits for them, and re-layouts  7.95 us (5%)
    pallas_call x1, Pallas kernels, fused(): pl.pallas_call(functools.partial(fused_kernel, cfg), out_shape=(pltpu.VME...  145 us
    unnamed x4, local copies, waits for them, and re-layouts  7.95 us

profile of v2, /device:TPU:0, one launch (start us, length us, event | category | flops | bytes accessed | tf_op | source)
XLA Modules:
  0.0 153.1 jit_solution(3517769085719406643)
XLA Ops:
  0.6 144.5 %shard_map.102 = (f32[896,2048]{1,0:T(8,128)S(1)}, f32[896,512]{1,0:T(8,128)S(1)}, bf16[896,2048]{1,0:T(8,128)(2,1)S(1)}, bf16[896,2048]{1,0:T(8,128)(2,1)S(1)}) custom-call(bf16[256,7168]{1,0:T(8,128)(2,1)} %hid.1, bf16[256,2048]{1,0:T(8,128)(2,1)} %og.1, f32[896,2048]{1,0:T(8,128)} %bitcast.7, bf16[896,2048]{1,0:T(8,128)(2,1)} %bitcast.8, ...), custom_call_target="tpu_custom_call" | custom-call | tf_op jit(solution)/shard_map/pallas_call | solution.py:600
  145.2 3.1 %copy.15 = f32[896,2048]{1,0:T(8,128)} copy(f32[896,2048]{1,0:T(8,128)S(1)} %get-tuple-element.12) | data formatting | bytes 14680064
  148.2 1.2 copy.16
  149.4 1.8 %copy.17 = bf16[1,896,2048]{2,1,0:T(8,128)(2,1)} copy(bf16[1,896,2048]{2,1,0:T(8,128)(2,1)S(1)} %bitcast.6) | data formatting | bytes 7340032
  151.3 1.8 %copy.18 = bf16[1,896,2048]{2,1,0:T(8,128)(2,1)} copy(bf16[1,896,2048]{2,1,0:T(8,128)(2,1)S(1)} %bitcast.5) | data formatting | bytes 7340032

commit v3 on v2

--- a/solution.py
+++ b/solution.py
@@ -216,8 +216,10 @@
 
 ROW_TILE = 128
 VMEM_BYTES = 40000000
+WRITE_BYTES = 20000000
 COL_TILE = 256
-HOP_STEPS = 5
+PIECE = COL_TILE // 2
+HOP_STEPS = 4
 AHEAD = 2
 SEGMENT_STEPS = 6
 LEAD = 1
@@ -225,17 +227,26 @@
 CODE_RANGE = 560.0
 
 
+def mod(x, k):
+    return x & (k - 1) if k & (k - 1) == 0 else x % k
+
+
+def div(x, k):
+    return x >> (k.bit_length() - 1) if k & (k - 1) == 0 else x // k
+
+
 def fused_kernel(
     cfg,
     hid, og, par_hbm, first_hbm, second_hbm, outer_hbm, mom_hbm,
     wide_ref, mom, first, second,
-    hbuf, ht, obuf, step, outer, out_ref, from_left, from_right,
+    hbuf, ht, obuf, step, outer, fresh, from_left, from_right,
     h_send, h_recv, o_send, o_recv, sib_send, sib_recv, load_sem,
     left_sem, right_sem, gather_sem, rs_send, ag_right, ag_left,
 ):
     n, peers, rows, width, tokens = cfg
     ni, nj = rows // ROW_TILE, width // COL_TILE
     stages = max(ni, nj)
+    pairs = n // 2
     halves = nj // n
     chips = peers // 2
     z = lax.axis_index("rep")
@@ -275,17 +286,26 @@
     ]
     starts = [sum(widths[:g]) for g in range(segments + 1)]
     total_steps = starts[-1]
-
-    def chunk_of(j):
-        return (j + (n - 1) * halves) % nj
+    even = 0
+    while even < segments - 1 and widths[even] == SEGMENT_STEPS:
+        even += 1
+    inverse = -(-65536 // SEGMENT_STEPS)
+    assert all(
+        min((u * inverse) >> 16, even) == min(u // SEGMENT_STEPS, even)
+        for u in range(total_steps)
+    )
+
+    def owner_of(j, h):
+        p = mod(j, pairs)
+        return pairs + p if h else pairs - 1 - p
 
     def own_lag(o):
         return max(o, n - 1 - o) if isinstance(o, int) else jnp.maximum(o, n - 1 - o)
 
     def place(u):
-        g = jnp.int32(0)
-        base = jnp.int32(0)
-        for a, b in zip(starts[:-2], starts[1:-1]):
+        g = jnp.minimum((u * inverse) >> 16, even)
+        base = g * SEGMENT_STEPS
+        for a, b in zip(starts[even:-2], starts[even + 1:-1]):
             past = flag(u >= b)
             g = g + past
             base = base + past * (b - a)
@@ -293,45 +313,47 @@
 
     def tile(u):
         g, q = place(u)
-        odd = g % 2
-        half = (g + 1) // 2
+        odd = g & 1
+        half = (g + 1) >> 1
         q = q - LEAD * odd
         i = jnp.where(odd == 1, q, half)
         j = jnp.where(odd == 1, half, q)
         valid = (u >= 0) & (u < total_steps) & (q >= 0) & (q < half + 1 - odd)
-        return valid, i, j, chunk_of(j)
+        return valid, i, j
 
     def rows_of(i):
         return pl.ds(pl.multiple_of(i * ROW_TILE, ROW_TILE), ROW_TILE)
 
-    def cols_of(c):
-        return pl.ds(pl.multiple_of(c * COL_TILE, COL_TILE), COL_TILE)
+    def piece_of(j):
+        return pl.ds(pl.multiple_of(div(j, pairs) * PIECE, PIECE), PIECE)
+
+    def cols_of(j, o):
+        start = o * (halves * COL_TILE) + div(j, pairs) * PIECE
+        return pl.ds(pl.multiple_of(start, PIECE), PIECE)
 
     def hid_cols(owner, s):
         return pl.ds(pl.multiple_of(owner * rows + s * ROW_TILE, ROW_TILE), ROW_TILE)
 
-    def send_o(s, d):
-        return pltpu.make_async_remote_copy(
-            src_ref=og.at[:, cols_of(chunk_of(s))],
-            dst_ref=obuf.at[s, me],
-            send_sem=o_send.at[s],
-            recv_sem=o_recv.at[s, chip],
-            device_id={"fsdp": peer_chip(d) * 2 + core},
-        )
-
     def issue_o(s):
-        for d in range(1, chips):
-            send_o(s, d).start()
-        pltpu.make_async_remote_copy(
-            src_ref=og.at[:, cols_of(chunk_of(s))],
-            dst_ref=obuf.at[s, me],
-            send_sem=sib_send.at[s],
-            recv_sem=sib_recv.at[s],
-            device_id={"fsdp": sibling},
-        ).start()
-        pltpu.make_async_copy(
-            og.at[:, cols_of(chunk_of(s))], obuf.at[s, me], o_recv.at[s, chip]
-        ).start()
+        for h in range(2):
+            source = og.at[:, cols_of(s, owner_of(s, h))]
+            target = obuf.at[s, me, :, pl.ds(h * PIECE, PIECE)]
+            for d in range(1, chips):
+                pltpu.make_async_remote_copy(
+                    src_ref=source,
+                    dst_ref=target,
+                    send_sem=o_send.at[s],
+                    recv_sem=o_recv.at[s, chip],
+                    device_id={"fsdp": peer_chip(d) * 2 + core},
+                ).start()
+            pltpu.make_async_remote_copy(
+                src_ref=source,
+                dst_ref=target,
+                send_sem=sib_send.at[s],
+                recv_sem=sib_recv.at[s],
+                device_id={"fsdp": sibling},
+            ).start()
+            pltpu.make_async_copy(source, target, o_recv.at[s, chip]).start()
 
     def forward_o(s):
         for d in range(chips):
@@ -402,77 +424,86 @@
     def decode(coded, terms):
         return jnp.log(coded.astype(jnp.float32)) * (1.0 / code_scale(terms))
 
-    def send_sum(i, j, o, to_right):
+    def send_sum(i, j, h, o, to_right):
         return pltpu.make_async_remote_copy(
-            src_ref=(from_left if to_right else from_right).at[i, j],
-            dst_ref=(from_left if to_right else from_right).at[i, j],
+            src_ref=(from_left if to_right else from_right).at[i, j, h],
+            dst_ref=(from_left if to_right else from_right).at[i, j, h],
             send_sem=rs_send.at[o],
-            recv_sem=(left_sem if to_right else right_sem).at[i, j],
+            recv_sem=(left_sem if to_right else right_sem).at[i, j, h],
             device_id={"rep": z + 1 if to_right else z - 1},
         )
 
-    def send_new(i, j, c, to_right):
-        at = rows_of(i), cols_of(c)
+    def send_new(i, j, h, o, to_right):
         return pltpu.make_async_remote_copy(
-            src_ref=out_ref.at[at],
-            dst_ref=out_ref.at[at],
-            send_sem=(ag_right if to_right else ag_left).at[c // halves],
-            recv_sem=gather_sem.at[i, j],
+            src_ref=fresh.at[i, j, h],
+            dst_ref=fresh.at[i, j, h],
+            send_sem=(ag_right if to_right else ag_left).at[o],
+            recv_sem=gather_sem.at[i, j, h],
             device_id={"rep": z + 1 if to_right else z - 1},
         )
 
     def wave(t, to_right):
         hop = z if to_right else n - 1 - z
-        valid, i, j, c = tile(t - hop * HOP_STEPS)
-        o = c // halves
-        beyond = (o > z) if to_right else (o < z)
-        at = rows_of(i), cols_of(c)
-        active = valid & beyond
+        valid, i, j = tile(t - hop * HOP_STEPS)
         partial = from_left if to_right else from_right
 
-        @pl.when(active & (hop == 0))
-        def _():
-            partial[i, j] = encode(step[at], hop + 1)
-            send_sum(i, j, o, to_right).start()
-
-        @pl.when(active & (hop > 0))
-        def _():
-            send_sum(i, j, o, to_right).wait_recv()
-            partial[i, j] = encode(decode(partial[i, j], hop) + step[at], hop + 1)
-            send_sum(i, j, o, to_right).start()
+        def piece(h):
+            o = owner_of(j, h)
+            active = valid & ((o > z) if to_right else (o < z))
+            at = rows_of(i), cols_of(j, o)
+
+            @pl.when(active & (hop == 0))
+            def _():
+                partial[i, j, h] = encode(step[at], hop + 1)
+                send_sum(i, j, h, o, to_right).start()
+
+            @pl.when(active & (hop > 0))
+            def _():
+                send_sum(i, j, h, o, to_right).wait_recv()
+                partial[i, j, h] = encode(decode(partial[i, j, h], hop) + step[at], hop + 1)
+                send_sum(i, j, h, o, to_right).start()
+
+        for h in (1, 0) if to_right else (0, 1):
+            piece(h)
+
+    def holds(j, o):
+        far = flag(o >= pairs)
+        match = jnp.where(far == 1, o - pairs, pairs - 1 - o) == mod(j, pairs)
+        return match, far
 
     def own(t):
-        valid, i, j, c = tile(t - own_lag(z) * HOP_STEPS)
-
-        @pl.when(valid & (c // halves == z))
-        def _():
-            at = rows_of(i), cols_of(c)
-            local = rows_of(i), cols_of(c % halves)
+        valid, i, j = tile(t - own_lag(z) * HOP_STEPS)
+        match, h = holds(j, z)
+
+        @pl.when(valid & match)
+        def _():
+            at = rows_of(i), cols_of(j, z)
+            local = rows_of(i), piece_of(j)
 
             @pl.when(has_left)
             def _():
-                send_sum(i, j, z, True).wait_recv()
-                step[at] += decode(from_left[i, j], z)
+                send_sum(i, j, h, z, True).wait_recv()
+                step[at] += decode(from_left[i, j, h], z)
 
             @pl.when(has_right)
             def _():
-                send_sum(i, j, z, False).wait_recv()
-                step[at] += decode(from_right[i, j], n - 1 - z)
+                send_sum(i, j, h, z, False).wait_recv()
+                step[at] += decode(from_right[i, j, h], n - 1 - z)
 
             delta = outer[local] - step[at] * (1.0 / n)
             momentum = nesterov * mom[local] + delta
             mom[local] = momentum
             updated = outer[local] - outer_rate * (delta + nesterov * momentum)
-            out_ref[at] = updated.astype(WIRE)
+            fresh[i, j, h] = updated.astype(WIRE)
             wide_ref[at] = updated
 
             @pl.when(has_right)
             def _():
-                send_new(i, j, c, True).start()
+                send_new(i, j, h, z, True).start()
 
             @pl.when(has_left)
             def _():
-                send_new(i, j, c, False).start()
+                send_new(i, j, h, z, False).start()
 
     def pass_on(t, e):
         o = (z + e) % n
@@ -480,62 +511,67 @@
         distance = jnp.where(to_right, z - o, o - z)
         edge = jnp.where(to_right, flag(has_right), flag(has_left)) == 0
         lag = (own_lag(o) + distance) * HOP_STEPS + EDGE_LAG * flag(edge)
-        valid, i, j, c = tile(t - lag)
-        ready = valid & (c // halves == o)
-        at = rows_of(i), cols_of(c)
-
-        @pl.when(ready)
-        def _():
-            send_new(i, j, c, True).wait_recv()
+        valid, i, j = tile(t - lag)
+        match, h = holds(j, o)
+        at = rows_of(i), cols_of(j, o)
+
+        @pl.when(valid & match)
+        def _():
+            send_new(i, j, h, o, True).wait_recv()
 
             @pl.when(to_right & has_right)
             def _():
-                send_new(i, j, c, True).start()
+                send_new(i, j, h, o, True).start()
 
             @pl.when((o > z) & has_left)
             def _():
-                send_new(i, j, c, False).start()
-
-            wide_ref[at] = out_ref[at].astype(jnp.float32)
+                send_new(i, j, h, o, False).start()
+
+            wide_ref[at] = fresh[i, j, h].astype(jnp.float32)
 
     def compute(t):
         g, q = place(t)
-        s = (g + 1) // 2
+        s = (g + 1) >> 1
         inside = t < total_steps
-        valid, i, j, c = tile(t)
-
-        @pl.when(inside & (g % 2 == 0) & (q == 0))
+        valid, i, j = tile(t)
+
+        @pl.when(inside & ((g & 1) == 0) & (q == 0))
         def _():
             issue(s + AHEAD)
             pltpu.make_async_copy(hbuf.at[s], hbuf.at[s], h_recv.at[s]).wait()
             ht[s] = hbuf[s].reshape(peers * tokens, ROW_TILE).T
 
-        @pl.when(inside & (g % 2 == 1) & (q == 0))
+        @pl.when(inside & ((g & 1) == 1) & (q == 0))
         def _():
             forward_o(s)
 
-        @pl.when(inside & (g % 2 == 1) & (q == LEAD))
+        @pl.when(inside & ((g & 1) == 1) & (q == LEAD))
         def _():
             gathered_o(s)
 
         @pl.when(valid)
         def _():
-            at = rows_of(i), cols_of(c)
-            gradient = jnp.dot(
+            gradients = jnp.dot(
                 ht[i],
                 obuf[j].reshape(peers * tokens, COL_TILE),
                 preferred_element_type=jnp.float32,
             )
-            one = beta_one * first[at].astype(jnp.float32) + (1.0 - beta_one) * gradient
-            two = beta_two * second[at].astype(jnp.float32) + (1.0 - beta_two) * gradient * gradient
-            first[at] = one.astype(jnp.bfloat16)
-            second[at] = two.astype(jnp.bfloat16)
-            corrected_one = one * (1.0 / (1.0 - beta_one**INNER_STEP))
-            corrected_two = two * (1.0 / (1.0 - beta_two**INNER_STEP))
-            held = step[at]
-            step[at] = held - inner_rate * (
-                corrected_one / (jnp.sqrt(corrected_two) + epsilon) + weight_decay * held
-            )
+            for h in range(2):
+                at = rows_of(i), cols_of(j, owner_of(j, h))
+                gradient = gradients[:, h * PIECE:(h + 1) * PIECE]
+                one = beta_one * first[at].astype(jnp.float32) + (1.0 - beta_one) * gradient
+                two = (
+                    beta_two * second[at].astype(jnp.float32)
+                    + (1.0 - beta_two) * gradient * gradient
+                )
+                first[at] = one.astype(jnp.bfloat16)
+                second[at] = two.astype(jnp.bfloat16)
+                corrected_one = one * (1.0 / (1.0 - beta_one**INNER_STEP))
+                corrected_two = two * (1.0 / (1.0 - beta_two**INNER_STEP))
+                held = step[at]
+                step[at] = held - inner_rate * (
+                    corrected_one / (jnp.sqrt(corrected_two) + epsilon) + weight_decay * held
+                )
 
     forward_o(0)
     for load in loads:
@@ -545,8 +581,7 @@
     last = 0
     for g, c in enumerate(counts):
         for q in range(c):
-            j = (g + 1) // 2 if g % 2 else q
-            o = chunk_of(j) // halves
+            o = owner_of((g + 1) // 2 if g % 2 else q, 0)
             hops = own_lag(o) + max(o, n - 1 - o)
             last = max(last, starts[g] + leads[g] + q + hops * HOP_STEPS + EDGE_LAG)
 
@@ -613,12 +648,12 @@
             pltpu.VMEM((nj, peers, tokens, COL_TILE), bf16),
             pltpu.VMEM((rows, width), f32),
             pltpu.VMEM((rows, block), f32),
-            pltpu.VMEM((rows, width), WIRE),
-            pltpu.VMEM((ni, nj, ROW_TILE, COL_TILE), WIRE),
-            pltpu.VMEM((ni, nj, ROW_TILE, COL_TILE), WIRE),
+            pltpu.VMEM((ni, nj, 2, ROW_TILE, PIECE), WIRE),
+            pltpu.VMEM((ni, nj, 2, ROW_TILE, PIECE), WIRE),
+            pltpu.VMEM((ni, nj, 2, ROW_TILE, PIECE), WIRE),
             dma((ni,)), dma((ni,)),
             dma((nj,)), dma((nj, peers // 2)), dma((nj,)), dma((nj,)), dma((5,)),
-            dma((ni, nj)), dma((ni, nj)), dma((ni, nj)),
+            dma((ni, nj, 2)), dma((ni, nj, 2)), dma((ni, nj, 2)),
             dma((n,)), dma((n,)), dma((n,)),
         ],
         compiler_params=pltpu.CompilerParams(
@@ -627,8 +662,31 @@
     )(hidden, out_grad, inner_params, first_moment, second_moment, outer_params, outer_momentum)
 
 
+def write_out_kernel(*refs):
+    count = (len(refs) - 1) // 2
+    sems = refs[-1]
+    copies = [
+        pltpu.make_async_copy(refs[k], refs[count + k], sems.at[k]) for k in range(count)
+    ]
+    for copy in copies:
+        copy.start()
+    for copy in copies:
+        copy.wait()
+
+
+def write_out(*arrays):
+    return pl.pallas_call(
+        write_out_kernel,
+        out_shape=tuple(jax.ShapeDtypeStruct(a.shape, a.dtype) for a in arrays),
+        in_specs=[pl.BlockSpec(memory_space=pltpu.VMEM)] * len(arrays),
+        out_specs=(pl.BlockSpec(memory_space=pl.ANY),) * len(arrays),
+        scratch_shapes=[pltpu.SemaphoreType.DMA((len(arrays),))],
+        compiler_params=pltpu.CompilerParams(vmem_limit_bytes=WRITE_BYTES),
+    )(*arrays)
+
+
 def fits(peers, n, rows, width, block, tokens):
-    if peers % 4 or rows % ROW_TILE or block % COL_TILE or tokens % 16:
+    if peers % 4 or n % 2 or rows % ROW_TILE or block % COL_TILE or tokens % 16:
         return False
     return 0 <= width // COL_TILE - rows // ROW_TILE <= 1
 
@@ -642,6 +700,9 @@
         gathered, new_momentum, new_first, new_second = fused(
             hidden, out_grad, inner_params[0], first_moment[0], second_moment[0],
             outer_params, outer_momentum,
+        )
+        gathered, new_momentum, new_first, new_second = write_out(
+            gathered, new_momentum, new_first, new_second
         )
         return gathered, new_momentum, new_first[None], new_second[None]
     columns = lax.all_to_all(hidden, "fsdp", split_axis=1, concat_axis=0, tiled=True)

time: 153 us -> 149 us (0.974)
  local copies, waits for them, and re-layouts: 7.95 us -> 0 us
  Pallas kernels: 145 us -> 148 us
    unnamed x4 -> x0, local copies, waits for them, and re-layouts: 7.95 us -> none
    pallas_call x0 -> x1, Pallas kernels: none -> 5.94 us  [write_out(): pl.pallas_call(write_out_kernel, out_shape=tuple((jax.ShapeDtypeStruct(a....]
    pallas_call x1, Pallas kernels: 145 us -> 142 us  [fused(): pl.pallas_call(functools.partial(fused_kernel, cfg), out_shape=(pltpu.VME...]
where the time goes in v3:
time: 149 us
  Pallas kernels  148 us (99%)
    pallas_call x1, Pallas kernels, fused(): pl.pallas_call(functools.partial(fused_kernel, cfg), out_shape=(pltpu.VME...  142 us
    pallas_call x1, Pallas kernels, write_out(): pl.pallas_call(write_out_kernel, out_shape=tuple((jax.ShapeDtypeStruct(a....  5.94 us

profile of v3, /device:TPU:0, one launch (start us, length us, event | category | flops | bytes accessed | tf_op | source)
XLA Modules:
  0.0 148.7 jit_solution(11705497463787242809)
XLA Ops:
  0.6 142.1 %shard_map.102 = (f32[896,2048]{1,0:T(8,128)S(1)}, f32[896,512]{1,0:T(8,128)S(1)}, bf16[896,2048]{1,0:T(8,128)(2,1)S(1)}, bf16[896,2048]{1,0:T(8,128)(2,1)S(1)}) custom-call(bf16[256,7168]{1,0:T(8,128)(2,1)} %hid.1, bf16[256,2048]{1,0:T(8,128)(2,1)} %og.1, f32[896,2048]{1,0:T(8,128)} %bitcast.5, bf16[896,2048]{1,0:T(8,128)(2,1)} %bitcast.6, ...), custom_call_target="tpu_custom_call" | custom-call | tf_op jit(solution)/shard_map/pallas_call | solution.py:635
  142.8 5.9 %shard_map.103 = (f32[896,2048]{1,0:T(8,128)}, f32[896,512]{1,0:T(8,128)}, bf16[896,2048]{1,0:T(8,128)(2,1)}, bf16[896,2048]{1,0:T(8,128)(2,1)}) custom-call(f32[896,2048]{1,0:T(8,128)S(1)} %get-tuple-element.12.refs_0_, f32[896,512]{1,0:T(8,128)S(1)} %get-tuple-element.13.refs_1_, bf16[896,2048]{1,0:T(8,128)(2,1)S(1)} %get-tuple-element.14.refs_2_, ...), custom_call_target="tpu_custom_call" | custom-call | tf_op jit(solution)/shard_map/pallas_call | solution.py:678
